TPU v7x, 32 devices: a whole 2x2x4 slice. The times are simulated.
32 devices in a mesh: dp: 8 (over z, y), section: 4 (over x, core).
Axes of the slice: x: 2, y: 2, z: 4, core: 2. Of those that a mesh axis runs over, the one named last changes fastest.
Arguments:
- patches: bfloat16 [64, 197, 1024], P('dp'), may hold values from -6 to 6
- ln1_gain: float32 [4, 1024], P('section'), may hold values from 0.5 to 1.5
- w_qkv: bfloat16 [4, 1024, 3072], P('section'), may hold values from -1 to 1
- w_out: bfloat16 [4, 1024, 1024], P('section'), may hold values from -0.1875 to 0.1875
- ln2_gain: float32 [4, 1024], P('section'), may hold values from 0.5 to 1.5
- w_fc1: bfloat16 [4, 1024, 2048], P('section'), may hold values from -0.1875 to 0.1875
- w_fc2: bfloat16 [4, 2048, 1024], P('section'), may hold values from -0.125 to 0.125
- final_norm_gain: float32 [1024], replicated, may hold values from 0.5 to 1.5
- w_head: bfloat16 [1024, 256], replicated, may hold values from -0.1875 to 0.1875
- online_embeddings: bfloat16 [64, 256], P('dp'), may hold values from -60 to 60
- queue: bfloat16 [32768, 256], P(('dp', 'section')), may hold values from -1 to 1, as said below
- owner: int32 [64], replicated, may hold values from 0 to 63, each once
- pointer: int32 [8], P('dp'), may hold values from 0 to 4088
Outputs:
- momentum_embeddings: bfloat16 [64, 256], P('dp')
- query_loss: float32 [64], P('dp')
- total_loss: float32 [], replicated
- new_queue: bfloat16 [32768, 256], P(('dp', 'section'))
Inputs may be any that keep to these rules, and one draw needn't show every extreme that they name: `queue`: every row has Euclidean norm below 1. Each value appears once: key j goes to group owner[j] // 8, so every group receives exactly 8 keys. `pointer`: first row of the group's shard where its new keys are written.
All inputs are finite; a program needn't handle non-finite values.
Results may differ from a plain program's by a relative error of at most 0.02.
Values may be sent and summed in bfloat16 or wider, within the bound.
No kernel may reach another device: no remote copies, remote signals or barrier semaphores. Data moves between devices by JAX's collectives and lax.ppermute only.
A program may use at most 128 MiB of HBM per device.

v0:
```python
import math
import jax
import jax.numpy as jnp
from jax import lax
from jax.sharding import PartitionSpec as P

HEADS = 16
HEAD_DIM = 64
TOKS = 197
IMG_MB = 2
contrastive_sharpness = 0.2


def from_behind(value, axis, steps):
    count = lax.axis_size(axis)
    initial, last = (max(0, -steps), min(count, count - steps))
    return lax.ppermute(value, axis, [(source, source + steps) for source in range(initial, last)])


def broadcast(value, axis, source):
    kept = jnp.where(lax.axis_index(axis) == source, value, 0).astype(value.dtype)
    return lax.psum(kept, axis)


def layer_norm(values, gain):
    center = values - jnp.mean(values, axis=-1, keepdims=True)
    spread = jnp.mean(center * center, axis=-1, keepdims=True)
    return center * lax.rsqrt(spread + 1e-06) * gain


def encoder_block(hidden, gain_one, qkv_weight, out_weight, gain_two, first_weight, second_weight):
    images = hidden.shape[0]
    width = hidden.shape[2]
    stream = hidden.astype(jnp.float32)
    normed = layer_norm(stream, gain_one).astype(jnp.bfloat16).reshape(images * TOKS, width)
    packed = jnp.dot(normed, qkv_weight, preferred_element_type=jnp.float32).astype(jnp.bfloat16)
    packed = packed.reshape(images, TOKS, 3, HEADS, HEAD_DIM)
    similarity_matrix = jnp.einsum(
        "bqhd,bkhd->bhqk", packed[:, :, 0], packed[:, :, 1], preferred_element_type=jnp.float32
    )
    similarity_matrix = similarity_matrix / math.sqrt(HEAD_DIM)
    peak = jnp.max(similarity_matrix, axis=-1, keepdims=True)
    expo = jnp.exp(similarity_matrix - peak)
    probs = (expo / jnp.sum(expo, axis=-1, keepdims=True)).astype(jnp.bfloat16)
    context = jnp.einsum(
        "bhqk,bkhd->bqhd", probs, packed[:, :, 2], preferred_element_type=jnp.float32
    )
    context = context.astype(jnp.bfloat16).reshape(images * TOKS, width)
    stream = stream + jnp.dot(context, out_weight, preferred_element_type=jnp.float32).reshape(
        images, TOKS, width
    )
    normed = layer_norm(stream, gain_two).astype(jnp.bfloat16).reshape(images * TOKS, width)
    inner = jax.nn.gelu(
        jnp.dot(normed, first_weight, preferred_element_type=jnp.float32), approximate=False
    )
    inner = inner.astype(jnp.bfloat16)
    stream = stream + jnp.dot(inner, second_weight, preferred_element_type=jnp.float32).reshape(
        images, TOKS, width
    )
    return stream.astype(jnp.bfloat16)


def key_head(class_rows, final_norm_gain, w_head):
    normed = layer_norm(class_rows.astype(jnp.float32), final_norm_gain).astype(jnp.bfloat16)
    projected = jnp.dot(normed, w_head, preferred_element_type=jnp.float32)
    scale = lax.rsqrt(1.0 + jnp.sum(projected * projected, axis=1, keepdims=True))
    return (projected * scale).astype(jnp.bfloat16)


def on_device(
    patches,
    ln1_gain,
    w_qkv,
    w_out,
    ln2_gain,
    w_fc1,
    w_fc2,
    final_norm_gain,
    w_head,
    online_embeddings,
    queue,
    owner,
    pointer,
):
    sections = lax.axis_size("section")
    section_index = lax.axis_index("section")
    group_index = lax.axis_index("dp")
    group_images = patches.shape[0]
    width = patches.shape[2]
    batch_size = IMG_MB // 2
    blocks = group_images // batch_size
    feeds = patches.reshape(blocks, batch_size, TOKS, width)

    def run_block(hidden):
        return encoder_block(
            hidden, ln1_gain[0], w_qkv[0], w_out[0], ln2_gain[0], w_fc1[0], w_fc2[0]
        )

    def keep_block(hidden):
        return hidden

    def advance(tick, carry):
        incoming, finished = carry
        fresh = lax.dynamic_index_in_dim(feeds, jnp.minimum(tick, blocks - 1), 0, keepdims=False)
        source = jnp.where(section_index == 0, fresh, incoming)
        active = jnp.logical_and(tick >= section_index, tick - section_index < blocks)
        result = lax.cond(active, run_block, keep_block, source)
        place = jnp.clip(tick - (sections - 1), 0, blocks - 1)
        stored = lax.dynamic_update_index_in_dim(finished, result[:, 0, :], place, 0)
        finished = jnp.where(tick >= sections - 1, stored, finished)
        passed = from_behind(result, "section", 1)
        return (passed, finished)

    start = (jnp.zeros_like(feeds[0]), jnp.zeros((blocks, batch_size, width), jnp.bfloat16))
    passed, finished = lax.fori_loop(0, blocks + sections - 1, advance, start)
    resident_embeddings = key_head(finished.reshape(group_images, width), final_norm_gain, w_head)
    momentum_embeddings = broadcast(resident_embeddings, "section", sections - 1)
    query_rows_full = lax.all_gather(online_embeddings, "dp", axis=0, tiled=True)
    share = queue.shape[0]
    similarity_matrix = (
        jnp.einsum("tw,fw->tf", query_rows_full, queue, preferred_element_type=jnp.float32)
        / contrastive_sharpness
    )
    local_peak = jnp.max(similarity_matrix, axis=1)
    top = lax.pmax(local_peak, ("dp", "section"))
    total = lax.psum(jnp.sum(jnp.exp(similarity_matrix - top[:, None]), axis=1), ("dp", "section"))
    negative_all = top + jnp.log(total)
    negative = lax.dynamic_slice_in_dim(negative_all, group_index * group_images, group_images, 0)
    matching_similarity = (
        jnp.sum(
            online_embeddings.astype(jnp.float32) * momentum_embeddings.astype(jnp.float32), axis=1
        )
        / contrastive_sharpness
    )
    larger = jnp.maximum(negative, matching_similarity)
    query_loss = (
        larger
        + jnp.log(jnp.exp(negative - larger) + jnp.exp(matching_similarity - larger))
        - matching_similarity
    )
    loss_sum = lax.psum(jnp.sum(query_loss), "dp")
    total_loss = loss_sum / (group_images * lax.axis_size("dp"))
    every_key = lax.all_gather(momentum_embeddings, "dp", axis=0, tiled=True)
    wanted = group_index * group_images + jnp.arange(group_images, dtype=jnp.int32)
    selector = (owner[None, :] == wanted[:, None]).astype(jnp.bfloat16)
    incoming_keys = jnp.dot(selector, every_key, preferred_element_type=jnp.float32).astype(
        jnp.bfloat16
    )
    row_place = section_index * share + jnp.arange(share, dtype=jnp.int32)
    slot_index = row_place - pointer[0]
    placing = (slot_index[:, None] == jnp.arange(group_images, dtype=jnp.int32)[None, :]).astype(
        jnp.bfloat16
    )
    written = jnp.dot(placing, incoming_keys, preferred_element_type=jnp.float32).astype(
        jnp.bfloat16
    )
    inside = jnp.logical_and(slot_index >= 0, slot_index < group_images)
    new_queue = jnp.where(inside[:, None], written, queue)
    return (momentum_embeddings, query_loss, total_loss, new_queue)


def solution(mesh):
    placed = (
        P("dp", None, None),
        P("section", None),
        P("section", None, None),
        P("section", None, None),
        P("section", None),
        P("section", None, None),
        P("section", None, None),
        P(),
        P(),
        P("dp", None),
        P(("dp", "section"), None),
        P(),
        P("dp"),
    )
    return jax.shard_map(
        on_device,
        mesh=mesh,
        in_specs=placed,
        out_specs=(P("dp", None), P("dp"), P(), P(("dp", "section"), None)),
        check_vma=False,
    )
```

profile of v0, /device:TPU:0, one launch (start us, length us, event | category | flops | bytes accessed | tf_op | source)
XLA Modules:
  0.0 522.6 jit_solution(10496831233054502232)
XLA Ops:
  6.2 320.3 %while.17 = (s32[]{:T(128)}, bf16[1,197,1024]{2,1,0:T(8,128)(2,1)S(1)}, bf16[8,1,1024]{2,1,0:T(2,128)(2,1)S(1)}, s32[]{:T(128)}, pred[]{:T(512)}, /*index=5*/bf1...) while((s32[]{:T(128)}, ...), condition=%wide.region_9.10_spmd, body=%wide.region_0.9_spmd.sunk | while | flops 3499673600 | bytes 49231128 | solution.py:115
  7.4 22.1 %conditional.2 = (bf16[1,197,1024]{2,1,0:T(8,128)(2,1)S(1)}) conditional(s32[]{:T(128)} %convert_element_type.128, bf16[1,197,1024]{2,1,0:T(8,128)(2,1)S(1)} %bitcast_select_fusion.2, (bf16[1,197,1024]{2,1,0:T(8,128)(2,1)S(1)}, f32[1,1024]{1,0:T(1,128)S(1)}, bf16[1,1024,3072]{2,1,0:T(8,128)(2,1)}, bf16[1,1024,1024]{2,1,0:T(8,128)(2,1)}, ...), branch_computations={%region_1.1_spmd, %region_2.8_spmd} | conditional | flops 3499470848 | bytes 46394252 | solution.py:107
  20.7 8.7 %fusion.40 = bf16[1,197,1024]{2,1,0:T(8,128)(2,1)S(1)} fusion(f32[1,197,1024]{2,1,0:T(8,128)S(1)} %get-tuple-element.344, bf16[1,2048,1024]{2,1,0:T(8,128)(2,1)} %get-tuple-element.295, bf16[1,1024,2048]{2,1,0:T(8,128)(2,1)} %get-tuple-element.294, f32[1024]{0:T(1024)S(1)} %bitcast.93, f32[197]{0:T(256)S(1)} %add_rsqrt_fusion, ...), kind=kOutput, calls=%fused_computation.40 | convolution fusion | flops 1679990784 | bytes 9604648 | tf_op jit(solution)/shard_map/while/body/eval_jaxpr/cond/branch_1_fun/dot_general | solution.py:57
  33.2 22.1 %conditional.2 = (bf16[1,197,1024]{2,1,0:T(8,128)(2,1)S(1)}) conditional(s32[]{:T(128)} %convert_element_type.128, bf16[1,197,1024]{2,1,0:T(8,128)(2,1)S(1)} %bitcast_select_fusion.2, (bf16[1,197,1024]{2,1,0:T(8,128)(2,1)S(1)}, f32[1,1024]{1,0:T(1,128)S(1)}, bf16[1,1024,3072]{2,1,0:T(8,128)(2,1)}, bf16[1,1024,1024]{2,1,0:T(8,128)(2,1)}, ...), branch_computations={%region_1.1_spmd, %region_2.8_spmd} | conditional | flops 3499470848 | bytes 46394252 | solution.py:107
  46.6 8.7 %fusion.40 = bf16[1,197,1024]{2,1,0:T(8,128)(2,1)S(1)} fusion(f32[1,197,1024]{2,1,0:T(8,128)S(1)} %get-tuple-element.344, bf16[1,2048,1024]{2,1,0:T(8,128)(2,1)} %get-tuple-element.295, bf16[1,1024,2048]{2,1,0:T(8,128)(2,1)} %get-tuple-element.294, f32[1024]{0:T(1024)S(1)} %bitcast.93, f32[197]{0:T(256)S(1)} %add_rsqrt_fusion, ...), kind=kOutput, calls=%fused_computation.40 | convolution fusion | flops 1679990784 | bytes 9604648 | tf_op jit(solution)/shard_map/while/body/eval_jaxpr/cond/branch_1_fun/dot_general | solution.py:57
  60.0 22.1 %conditional.2 = (bf16[1,197,1024]{2,1,0:T(8,128)(2,1)S(1)}) conditional(s32[]{:T(128)} %convert_element_type.128, bf16[1,197,1024]{2,1,0:T(8,128)(2,1)S(1)} %bitcast_select_fusion.2, (bf16[1,197,1024]{2,1,0:T(8,128)(2,1)S(1)}, f32[1,1024]{1,0:T(1,128)S(1)}, bf16[1,1024,3072]{2,1,0:T(8,128)(2,1)}, bf16[1,1024,1024]{2,1,0:T(8,128)(2,1)}, ...), branch_computations={%region_1.1_spmd, %region_2.8_spmd} | conditional | flops 3499470848 | bytes 46394252 | solution.py:107
  73.4 8.7 %fusion.40 = bf16[1,197,1024]{2,1,0:T(8,128)(2,1)S(1)} fusion(f32[1,197,1024]{2,1,0:T(8,128)S(1)} %get-tuple-element.344, bf16[1,2048,1024]{2,1,0:T(8,128)(2,1)} %get-tuple-element.295, bf16[1,1024,2048]{2,1,0:T(8,128)(2,1)} %get-tuple-element.294, f32[1024]{0:T(1024)S(1)} %bitcast.93, f32[197]{0:T(256)S(1)} %add_rsqrt_fusion, ...), kind=kOutput, calls=%fused_computation.40 | convolution fusion | flops 1679990784 | bytes 9604648 | tf_op jit(solution)/shard_map/while/body/eval_jaxpr/cond/branch_1_fun/dot_general | solution.py:57
  82.2 5.5 %collective-permute-start = (bf16[1,197,1024]{2,1,0:T(8,128)(2,1)S(1)}, bf16[1,197,1024]{2,1,0:T(8,128)(2,1)S(1)}, u32[]{:S(2)}, u32[]{:S(2)}) collective-permute-start(bf16[1,197,1024]{2,1,0:T(8,128)(2,1)S(1)} %get-tuple-element.476), channel_id=1, source_target_pairs={{0,1},{1,2},{2,3},{4,5},{5,6},{6,7},{8,9},{9,10},{10,11},{12,13},{... | collective-permute-start | bytes 1210376 | tf_op jit(solution)/shard_map/while/body/eval_jaxpr/ppermute | solution.py:17
  90.0 22.1 %conditional.2 = (bf16[1,197,1024]{2,1,0:T(8,128)(2,1)S(1)}) conditional(s32[]{:T(128)} %convert_element_type.128, bf16[1,197,1024]{2,1,0:T(8,128)(2,1)S(1)} %bitcast_select_fusion.2, (bf16[1,197,1024]{2,1,0:T(8,128)(2,1)S(1)}, f32[1,1024]{1,0:T(1,128)S(1)}, bf16[1,1024,3072]{2,1,0:T(8,128)(2,1)}, bf16[1,1024,1024]{2,1,0:T(8,128)(2,1)}, ...), branch_computations={%region_1.1_spmd, %region_2.8_spmd} | conditional | flops 3499470848 | bytes 46394252 | solution.py:107
  103.4 8.7 %fusion.40 = bf16[1,197,1024]{2,1,0:T(8,128)(2,1)S(1)} fusion(f32[1,197,1024]{2,1,0:T(8,128)S(1)} %get-tuple-element.344, bf16[1,2048,1024]{2,1,0:T(8,128)(2,1)} %get-tuple-element.295, bf16[1,1024,2048]{2,1,0:T(8,128)(2,1)} %get-tuple-element.294, f32[1024]{0:T(1024)S(1)} %bitcast.93, f32[197]{0:T(256)S(1)} %add_rsqrt_fusion, ...), kind=kOutput, calls=%fused_computation.40 | convolution fusion | flops 1679990784 | bytes 9604648 | tf_op jit(solution)/shard_map/while/body/eval_jaxpr/cond/branch_1_fun/dot_general | solution.py:57
  112.2 7.9 %collective-permute-start = (bf16[1,197,1024]{2,1,0:T(8,128)(2,1)S(1)}, bf16[1,197,1024]{2,1,0:T(8,128)(2,1)S(1)}, u32[]{:S(2)}, u32[]{:S(2)}) collective-permute-start(bf16[1,197,1024]{2,1,0:T(8,128)(2,1)S(1)} %get-tuple-element.476), channel_id=1, source_target_pairs={{0,1},{1,2},{2,3},{4,5},{5,6},{6,7},{8,9},{9,10},{10,11},{12,13},{... | collective-permute-start | bytes 1210376 | tf_op jit(solution)/shard_map/while/body/eval_jaxpr/ppermute | solution.py:17
  122.5 22.1 %conditional.2 = (bf16[1,197,1024]{2,1,0:T(8,128)(2,1)S(1)}) conditional(s32[]{:T(128)} %convert_element_type.128, bf16[1,197,1024]{2,1,0:T(8,128)(2,1)S(1)} %bitcast_select_fusion.2, (bf16[1,197,1024]{2,1,0:T(8,128)(2,1)S(1)}, f32[1,1024]{1,0:T(1,128)S(1)}, bf16[1,1024,3072]{2,1,0:T(8,128)(2,1)}, bf16[1,1024,1024]{2,1,0:T(8,128)(2,1)}, ...), branch_computations={%region_1.1_spmd, %region_2.8_spmd} | conditional | flops 3499470848 | bytes 46394252 | solution.py:107
  135.9 8.7 %fusion.40 = bf16[1,197,1024]{2,1,0:T(8,128)(2,1)S(1)} fusion(f32[1,197,1024]{2,1,0:T(8,128)S(1)} %get-tuple-element.344, bf16[1,2048,1024]{2,1,0:T(8,128)(2,1)} %get-tuple-element.295, bf16[1,1024,2048]{2,1,0:T(8,128)(2,1)} %get-tuple-element.294, f32[1024]{0:T(1024)S(1)} %bitcast.93, f32[197]{0:T(256)S(1)} %add_rsqrt_fusion, ...), kind=kOutput, calls=%fused_computation.40 | convolution fusion | flops 1679990784 | bytes 9604648 | tf_op jit(solution)/shard_map/while/body/eval_jaxpr/cond/branch_1_fun/dot_general | solution.py:57
  144.6 7.9 %collective-permute-start = (bf16[1,197,1024]{2,1,0:T(8,128)(2,1)S(1)}, bf16[1,197,1024]{2,1,0:T(8,128)(2,1)S(1)}, u32[]{:S(2)}, u32[]{:S(2)}) collective-permute-start(bf16[1,197,1024]{2,1,0:T(8,128)(2,1)S(1)} %get-tuple-element.476), channel_id=1, source_target_pairs={{0,1},{1,2},{2,3},{4,5},{5,6},{6,7},{8,9},{9,10},{10,11},{12,13},{... | collective-permute-start | bytes 1210376 | tf_op jit(solution)/shard_map/while/body/eval_jaxpr/ppermute | solution.py:17
  154.9 22.1 %conditional.2 = (bf16[1,197,1024]{2,1,0:T(8,128)(2,1)S(1)}) conditional(s32[]{:T(128)} %convert_element_type.128, bf16[1,197,1024]{2,1,0:T(8,128)(2,1)S(1)} %bitcast_select_fusion.2, (bf16[1,197,1024]{2,1,0:T(8,128)(2,1)S(1)}, f32[1,1024]{1,0:T(1,128)S(1)}, bf16[1,1024,3072]{2,1,0:T(8,128)(2,1)}, bf16[1,1024,1024]{2,1,0:T(8,128)(2,1)}, ...), branch_computations={%region_1.1_spmd, %region_2.8_spmd} | conditional | flops 3499470848 | bytes 46394252 | solution.py:107
  168.3 8.7 %fusion.40 = bf16[1,197,1024]{2,1,0:T(8,128)(2,1)S(1)} fusion(f32[1,197,1024]{2,1,0:T(8,128)S(1)} %get-tuple-element.344, bf16[1,2048,1024]{2,1,0:T(8,128)(2,1)} %get-tuple-element.295, bf16[1,1024,2048]{2,1,0:T(8,128)(2,1)} %get-tuple-element.294, f32[1024]{0:T(1024)S(1)} %bitcast.93, f32[197]{0:T(256)S(1)} %add_rsqrt_fusion, ...), kind=kOutput, calls=%fused_computation.40 | convolution fusion | flops 1679990784 | bytes 9604648 | tf_op jit(solution)/shard_map/while/body/eval_jaxpr/cond/branch_1_fun/dot_general | solution.py:57
  177.1 7.9 %collective-permute-start = (bf16[1,197,1024]{2,1,0:T(8,128)(2,1)S(1)}, bf16[1,197,1024]{2,1,0:T(8,128)(2,1)S(1)}, u32[]{:S(2)}, u32[]{:S(2)}) collective-permute-start(bf16[1,197,1024]{2,1,0:T(8,128)(2,1)S(1)} %get-tuple-element.476), channel_id=1, source_target_pairs={{0,1},{1,2},{2,3},{4,5},{5,6},{6,7},{8,9},{9,10},{10,11},{12,13},{... | collective-permute-start | bytes 1210376 | tf_op jit(solution)/shard_map/while/body/eval_jaxpr/ppermute | solution.py:17
  187.4 22.1 %conditional.2 = (bf16[1,197,1024]{2,1,0:T(8,128)(2,1)S(1)}) conditional(s32[]{:T(128)} %convert_element_type.128, bf16[1,197,1024]{2,1,0:T(8,128)(2,1)S(1)} %bitcast_select_fusion.2, (bf16[1,197,1024]{2,1,0:T(8,128)(2,1)S(1)}, f32[1,1024]{1,0:T(1,128)S(1)}, bf16[1,1024,3072]{2,1,0:T(8,128)(2,1)}, bf16[1,1024,1024]{2,1,0:T(8,128)(2,1)}, ...), branch_computations={%region_1.1_spmd, %region_2.8_spmd} | conditional | flops 3499470848 | bytes 46394252 | solution.py:107
  200.8 8.7 %fusion.40 = bf16[1,197,1024]{2,1,0:T(8,128)(2,1)S(1)} fusion(f32[1,197,1024]{2,1,0:T(8,128)S(1)} %get-tuple-element.344, bf16[1,2048,1024]{2,1,0:T(8,128)(2,1)} %get-tuple-element.295, bf16[1,1024,2048]{2,1,0:T(8,128)(2,1)} %get-tuple-element.294, f32[1024]{0:T(1024)S(1)} %bitcast.93, f32[197]{0:T(256)S(1)} %add_rsqrt_fusion, ...), kind=kOutput, calls=%fused_computation.40 | convolution fusion | flops 1679990784 | bytes 9604648 | tf_op jit(solution)/shard_map/while/body/eval_jaxpr/cond/branch_1_fun/dot_general | solution.py:57
  209.5 7.9 %collective-permute-start = (bf16[1,197,1024]{2,1,0:T(8,128)(2,1)S(1)}, bf16[1,197,1024]{2,1,0:T(8,128)(2,1)S(1)}, u32[]{:S(2)}, u32[]{:S(2)}) collective-permute-start(bf16[1,197,1024]{2,1,0:T(8,128)(2,1)S(1)} %get-tuple-element.476), channel_id=1, source_target_pairs={{0,1},{1,2},{2,3},{4,5},{5,6},{6,7},{8,9},{9,10},{10,11},{12,13},{... | collective-permute-start | bytes 1210376 | tf_op jit(solution)/shard_map/while/body/eval_jaxpr/ppermute | solution.py:17
  219.8 22.1 %conditional.2 = (bf16[1,197,1024]{2,1,0:T(8,128)(2,1)S(1)}) conditional(s32[]{:T(128)} %convert_element_type.128, bf16[1,197,1024]{2,1,0:T(8,128)(2,1)S(1)} %bitcast_select_fusion.2, (bf16[1,197,1024]{2,1,0:T(8,128)(2,1)S(1)}, f32[1,1024]{1,0:T(1,128)S(1)}, bf16[1,1024,3072]{2,1,0:T(8,128)(2,1)}, bf16[1,1024,1024]{2,1,0:T(8,128)(2,1)}, ...), branch_computations={%region_1.1_spmd, %region_2.8_spmd} | conditional | flops 3499470848 | bytes 46394252 | solution.py:107
  233.2 8.7 %fusion.40 = bf16[1,197,1024]{2,1,0:T(8,128)(2,1)S(1)} fusion(f32[1,197,1024]{2,1,0:T(8,128)S(1)} %get-tuple-element.344, bf16[1,2048,1024]{2,1,0:T(8,128)(2,1)} %get-tuple-element.295, bf16[1,1024,2048]{2,1,0:T(8,128)(2,1)} %get-tuple-element.294, f32[1024]{0:T(1024)S(1)} %bitcast.93, f32[197]{0:T(256)S(1)} %add_rsqrt_fusion, ...), kind=kOutput, calls=%fused_computation.40 | convolution fusion | flops 1679990784 | bytes 9604648 | tf_op jit(solution)/shard_map/while/body/eval_jaxpr/cond/branch_1_fun/dot_general | solution.py:57
  242.0 7.9 %collective-permute-start = (bf16[1,197,1024]{2,1,0:T(8,128)(2,1)S(1)}, bf16[1,197,1024]{2,1,0:T(8,128)(2,1)S(1)}, u32[]{:S(2)}, u32[]{:S(2)}) collective-permute-start(bf16[1,197,1024]{2,1,0:T(8,128)(2,1)S(1)} %get-tuple-element.476), channel_id=1, source_target_pairs={{0,1},{1,2},{2,3},{4,5},{5,6},{6,7},{8,9},{9,10},{10,11},{12,13},{... | collective-permute-start | bytes 1210376 | tf_op jit(solution)/shard_map/while/body/eval_jaxpr/ppermute | solution.py:17
  252.3 30.1 %collective-permute-start = (bf16[1,197,1024]{2,1,0:T(8,128)(2,1)S(1)}, bf16[1,197,1024]{2,1,0:T(8,128)(2,1)S(1)}, u32[]{:S(2)}, u32[]{:S(2)}) collective-permute-start(bf16[1,197,1024]{2,1,0:T(8,128)(2,1)S(1)} %get-tuple-element.476), channel_id=1, source_target_pairs={{0,1},{1,2},{2,3},{4,5},{5,6},{6,7},{8,9},{9,10},{10,11},{12,13},{... | collective-permute-start | bytes 1210376 | tf_op jit(solution)/shard_map/while/body/eval_jaxpr/ppermute | solution.py:17
  284.8 7.9 %collective-permute-start = (bf16[1,197,1024]{2,1,0:T(8,128)(2,1)S(1)}, bf16[1,197,1024]{2,1,0:T(8,128)(2,1)S(1)}, u32[]{:S(2)}, u32[]{:S(2)}) collective-permute-start(bf16[1,197,1024]{2,1,0:T(8,128)(2,1)S(1)} %get-tuple-element.476), channel_id=1, source_target_pairs={{0,1},{1,2},{2,3},{4,5},{5,6},{6,7},{8,9},{9,10},{10,11},{12,13},{... | collective-permute-start | bytes 1210376 | tf_op jit(solution)/shard_map/while/body/eval_jaxpr/ppermute | solution.py:17
  295.1 30.1 %collective-permute-start = (bf16[1,197,1024]{2,1,0:T(8,128)(2,1)S(1)}, bf16[1,197,1024]{2,1,0:T(8,128)(2,1)S(1)}, u32[]{:S(2)}, u32[]{:S(2)}) collective-permute-start(bf16[1,197,1024]{2,1,0:T(8,128)(2,1)S(1)} %get-tuple-element.476), channel_id=1, source_target_pairs={{0,1},{1,2},{2,3},{4,5},{5,6},{6,7},{8,9},{9,10},{10,11},{12,13},{... | collective-permute-start | bytes 1210376 | tf_op jit(solution)/shard_map/while/body/eval_jaxpr/ppermute | solution.py:17
  327.3 24.5 %psum.21 = bf16[8,256]{1,0:T(8,128)(2,1)S(1)} all-reduce(bf16[8,256]{1,0:T(8,128)(2,1)S(1)} %fusion.136), channel_id=1, replica_groups=mesh['dp'=8,'section'=4] {'section'}, use_global_device_ids=true, to_apply=%region_13.14 | all-reduce | flops 2048 | bytes 8192 | tf_op jit(solution)/shard_map/psum | solution.py:22
  351.8 32.6 %all_gather.7 = bf16[64,256]{1,0:T(8,128)(2,1)S(1)} all-gather(bf16[8,256]{1,0:T(8,128)(2,1)S(1)} %psum.21), channel_id=1, replica_groups=mesh['dp'=8,'section'=4] {'dp'}, dimensions={0}, use_global_device_ids=true | all-gather | bytes 36864 | tf_op jit(solution)/shard_map/all_gather | solution.py:143
  386.5 30.6 %all_gather.6 = bf16[64,256]{1,0:T(8,128)(2,1)S(1)} all-gather(bf16[8,256]{1,0:T(8,128)(2,1)S(1)} %copy-done.4), channel_id=1, replica_groups=mesh['dp'=8,'section'=4] {'dp'}, dimensions={0}, use_global_device_ids=true | all-gather | bytes 36864 | tf_op jit(solution)/shard_map/all_gather | solution.py:118
  417.5 38.5 %pmax.7 = f32[64]{0:T(128)S(1)} all-reduce(f32[64]{0:T(128)S(1)} %get-tuple-element.347), channel_id=1, replica_groups=mesh['dp'=8,'section'=4] {'dp','section'}, use_global_device_ids=true, to_apply=%region_15.16 | all-reduce | flops 64 | bytes 512 | tf_op jit(solution)/shard_map/pmax | solution.py:125
  456.3 41.6 %psum.22 = f32[64]{0:T(128)S(1)} all-reduce(f32[64]{0:T(128)S(1)} %exponential_reduce_fusion), channel_id=1, replica_groups=mesh['dp'=8,'section'=4] {'dp','section'}, use_global_device_ids=true, to_apply=%region_17.18 | all-reduce | flops 64 | bytes 512 | tf_op jit(solution)/shard_map/psum | solution.py:126
  499.1 21.7 %psum.23 = f32[]{:T(128)} all-reduce(f32[]{:T(128)} %get-tuple-element.339), channel_id=1, replica_groups=mesh['dp'=8,'section'=4] {'dp'}, use_global_device_ids=true, to_apply=%region_20.21 | all-reduce | flops 1 | bytes 8 | tf_op jit(solution)/shard_map/psum | solution.py:141
  (194 shorter events, 145.8 us)
Async XLA Ops:
  0.6 326.3 %copy-start = (bf16[1024,256]{1,0:T(8,128)(2,1)S(1)}, bf16[1024,256]{1,0:T(8,128)(2,1)}, u32[]{:S(2)}) copy-start(bf16[1024,256]{1,0:T(8,128)(2,1)} %param.25) | copy-start | bytes 1572868
  0.7 5.5 %copy-start.6 = (f32[1,1024]{1,0:T(1,128)S(1)}, f32[1,1024]{1,0:T(1,128)}, u32[]{:S(2)}) copy-start(f32[1,1024]{1,0:T(1,128)} %param.18) | copy-start | bytes 12292
  0.7 5.5 %copy-start.7 = (f32[1,1024]{1,0:T(1,128)S(1)}, f32[1,1024]{1,0:T(1,128)}, u32[]{:S(2)}) copy-start(f32[1,1024]{1,0:T(1,128)} %param.21) | copy-start | bytes 12292
  6.2 320.7 %copy-start.8 = (f32[1024]{0:T(1024)S(1)}, f32[1024]{0:T(1024)}, u32[]{:S(2)}) copy-start(f32[1024]{0:T(1024)} %param.24) | copy-start | bytes 12292
  6.2 378.9 %copy-start.2 = (bf16[1024,256]{1,0:T(8,128)(2,1)S(1)}, bf16[1024,256]{1,0:T(8,128)(2,1)}, u32[]{:S(2)}) copy-start(bf16[1024,256]{1,0:T(8,128)(2,1)} %param.27) | copy-start | bytes 1572868
  6.2 378.9 %copy-start.5 = (s32[64]{0:T(128)S(1)}, s32[64]{0:T(128)}, u32[]{:S(2)}) copy-start(s32[64]{0:T(128)} %param.28) | copy-start | bytes 772
  18.2 1.6 copy-start.1
  29.5 2.7 collective-permute-start
  44.0 1.6 copy-start.1
  55.3 3.7 collective-permute-start
  70.9 1.6 copy-start.1
  82.2 6.8 %collective-permute-start = (bf16[1,197,1024]{2,1,0:T(8,128)(2,1)S(1)}, bf16[1,197,1024]{2,1,0:T(8,128)(2,1)S(1)}, u32[]{:S(2)}, u32[]{:S(2)}) collective-permute-start(bf16[1,197,1024]{2,1,0:T(8,128)(2,1)S(1)} %get-tuple-element.476), channel_id=1, source_target_pairs={{0,1},{1,2},{2,3},{4,5},{5,6},{6,7},{8,9},{9,10},{10,11},{12,13},{... | collective-permute-start | bytes 1210376 | tf_op jit(solution)/shard_map/while/body/eval_jaxpr/ppermute | solution.py:17
  100.9 1.6 copy-start.1
  112.2 9.3 %collective-permute-start = (bf16[1,197,1024]{2,1,0:T(8,128)(2,1)S(1)}, bf16[1,197,1024]{2,1,0:T(8,128)(2,1)S(1)}, u32[]{:S(2)}, u32[]{:S(2)}) collective-permute-start(bf16[1,197,1024]{2,1,0:T(8,128)(2,1)S(1)} %get-tuple-element.476), channel_id=1, source_target_pairs={{0,1},{1,2},{2,3},{4,5},{5,6},{6,7},{8,9},{9,10},{10,11},{12,13},{... | collective-permute-start | bytes 1210376 | tf_op jit(solution)/shard_map/while/body/eval_jaxpr/ppermute | solution.py:17
  133.3 1.6 copy-start.1
  144.6 9.3 %collective-permute-start = (bf16[1,197,1024]{2,1,0:T(8,128)(2,1)S(1)}, bf16[1,197,1024]{2,1,0:T(8,128)(2,1)S(1)}, u32[]{:S(2)}, u32[]{:S(2)}) collective-permute-start(bf16[1,197,1024]{2,1,0:T(8,128)(2,1)S(1)} %get-tuple-element.476), channel_id=1, source_target_pairs={{0,1},{1,2},{2,3},{4,5},{5,6},{6,7},{8,9},{9,10},{10,11},{12,13},{... | collective-permute-start | bytes 1210376 | tf_op jit(solution)/shard_map/while/body/eval_jaxpr/ppermute | solution.py:17
  165.8 1.6 copy-start.1
  177.1 9.3 %collective-permute-start = (bf16[1,197,1024]{2,1,0:T(8,128)(2,1)S(1)}, bf16[1,197,1024]{2,1,0:T(8,128)(2,1)S(1)}, u32[]{:S(2)}, u32[]{:S(2)}) collective-permute-start(bf16[1,197,1024]{2,1,0:T(8,128)(2,1)S(1)} %get-tuple-element.476), channel_id=1, source_target_pairs={{0,1},{1,2},{2,3},{4,5},{5,6},{6,7},{8,9},{9,10},{10,11},{12,13},{... | collective-permute-start | bytes 1210376 | tf_op jit(solution)/shard_map/while/body/eval_jaxpr/ppermute | solution.py:17
  198.2 1.6 copy-start.1
  209.5 9.3 %collective-permute-start = (bf16[1,197,1024]{2,1,0:T(8,128)(2,1)S(1)}, bf16[1,197,1024]{2,1,0:T(8,128)(2,1)S(1)}, u32[]{:S(2)}, u32[]{:S(2)}) collective-permute-start(bf16[1,197,1024]{2,1,0:T(8,128)(2,1)S(1)} %get-tuple-element.476), channel_id=1, source_target_pairs={{0,1},{1,2},{2,3},{4,5},{5,6},{6,7},{8,9},{9,10},{10,11},{12,13},{... | collective-permute-start | bytes 1210376 | tf_op jit(solution)/shard_map/while/body/eval_jaxpr/ppermute | solution.py:17
  230.7 1.6 copy-start.1
  242.0 9.3 %collective-permute-start = (bf16[1,197,1024]{2,1,0:T(8,128)(2,1)S(1)}, bf16[1,197,1024]{2,1,0:T(8,128)(2,1)S(1)}, u32[]{:S(2)}, u32[]{:S(2)}) collective-permute-start(bf16[1,197,1024]{2,1,0:T(8,128)(2,1)S(1)} %get-tuple-element.476), channel_id=1, source_target_pairs={{0,1},{1,2},{2,3},{4,5},{5,6},{6,7},{8,9},{9,10},{10,11},{12,13},{... | collective-permute-start | bytes 1210376 | tf_op jit(solution)/shard_map/while/body/eval_jaxpr/ppermute | solution.py:17
  252.3 31.4 %collective-permute-start = (bf16[1,197,1024]{2,1,0:T(8,128)(2,1)S(1)}, bf16[1,197,1024]{2,1,0:T(8,128)(2,1)S(1)}, u32[]{:S(2)}, u32[]{:S(2)}) collective-permute-start(bf16[1,197,1024]{2,1,0:T(8,128)(2,1)S(1)} %get-tuple-element.476), channel_id=1, source_target_pairs={{0,1},{1,2},{2,3},{4,5},{5,6},{6,7},{8,9},{9,10},{10,11},{12,13},{... | collective-permute-start | bytes 1210376 | tf_op jit(solution)/shard_map/while/body/eval_jaxpr/ppermute | solution.py:17
  284.8 9.3 %collective-permute-start = (bf16[1,197,1024]{2,1,0:T(8,128)(2,1)S(1)}, bf16[1,197,1024]{2,1,0:T(8,128)(2,1)S(1)}, u32[]{:S(2)}, u32[]{:S(2)}) collective-permute-start(bf16[1,197,1024]{2,1,0:T(8,128)(2,1)S(1)} %get-tuple-element.476), channel_id=1, source_target_pairs={{0,1},{1,2},{2,3},{4,5},{5,6},{6,7},{8,9},{9,10},{10,11},{12,13},{... | collective-permute-start | bytes 1210376 | tf_op jit(solution)/shard_map/while/body/eval_jaxpr/ppermute | solution.py:17
  295.1 31.4 %collective-permute-start = (bf16[1,197,1024]{2,1,0:T(8,128)(2,1)S(1)}, bf16[1,197,1024]{2,1,0:T(8,128)(2,1)S(1)}, u32[]{:S(2)}, u32[]{:S(2)}) collective-permute-start(bf16[1,197,1024]{2,1,0:T(8,128)(2,1)S(1)} %get-tuple-element.476), channel_id=1, source_target_pairs={{0,1},{1,2},{2,3},{4,5},{5,6},{6,7},{8,9},{9,10},{10,11},{12,13},{... | collective-permute-start | bytes 1210376 | tf_op jit(solution)/shard_map/while/body/eval_jaxpr/ppermute | solution.py:17
  326.5 59.9 %copy-start.4 = (bf16[8,256]{1,0:T(8,128)(2,1)S(1)}, bf16[8,256]{1,0:T(8,128)(2,1)}, u32[]{:S(2)}) copy-start(bf16[8,256]{1,0:T(8,128)(2,1)} %param.26) | copy-start | bytes 12292
  351.8 169.6 %copy-start.3 = (bf16[8,256]{1,0:T(8,128)(2,1)}, bf16[8,256]{1,0:T(8,128)(2,1)S(1)}, u32[]{:S(2)}) copy-start(bf16[8,256]{1,0:T(8,128)(2,1)S(1)} %psum.21) | copy-start | bytes 12292
where the time goes:
time: 524 us; the launch traced here: 523 us
  blocking collectives  190 us (36%)
  matrix products  130 us (25%)
  starting transfers between devices  117 us (22%)
  other arithmetic  40.6 us (8%)
  local copies, waits for them, and re-layouts  27.6 us (5%)
  waiting for transfers between devices  14.3 us (3%)
    ppermute x11, starting transfers between devices, from_behind(): lax.ppermute(value, axis, [(source, source + steps) for source in range(i...  117 us
    dot_general x8, matrix products, encoder_block(): jnp.dot(inner, second_weight, preferred_element_type=jnp.float32)  70 us
    dot_general x8, matrix products, encoder_block(): jnp.dot(normed, qkv_weight, preferred_element_type=jnp.float32)  43.2 us
    psum x1, blocking collectives, on_device(): lax.psum(jnp.sum(jnp.exp(similarity_matrix - top[:, None]), axis=1), ('dp...  41.6 us
    pmax x1, blocking collectives, on_device(): top = lax.pmax(local_peak, ('dp', 'section'))  38.5 us
    all_gather x1, blocking collectives, on_device(): every_key = lax.all_gather(momentum_embeddings, 'dp', axis=0, tiled=True)  32.6 us
    all_gather x1, blocking collectives, on_device(): lax.all_gather(online_embeddings, 'dp', axis=0, tiled=True)  30.6 us
    psum x1, blocking collectives, broadcast(): return lax.psum(kept, axis)  24.5 us
  transfers between devices with their start and end apart: 11, of which 11 were waited for; matrix products, arithmetic and copies ran while one was open for 0% of the time, Pallas kernels for 0%

commit v1 on v0

--- a/solution.py
+++ b/solution.py
@@ -3,12 +3,35 @@
 import jax.numpy as jnp
 from jax import lax
 from jax.sharding import PartitionSpec as P
+from jax.lax import axis_index, axis_size, ppermute
 
 HEADS = 16
 HEAD_DIM = 64
 TOKS = 197
 IMG_MB = 2
 contrastive_sharpness = 0.2
+
+
+def lay_group_by_axis(work_x, named_axis, packet):
+    next_value = axis_size(named_axis)
+    frame_out = axis_index(named_axis)
+    state_now, local_now, main = (next_value, frame_out, work_x.shape[0])
+    row_list = [(no, (no + 1) % state_now) for no in range(state_now)]
+    prior, piece_out = (work_x, None)
+    c = 0
+    while c < state_now:
+        item_now = (local_now - c) % state_now
+        arr_now = ppermute(prior, named_axis, row_list) if c < state_now - 1 else None
+        x_new = packet(prior, item_now * main)
+        then = x_new.shape[0]
+        if piece_out is None:
+            piece_out = jnp.zeros(
+                (*x_new.shape[:0], state_now * then, *x_new.shape[1:]), x_new.dtype
+            )
+        piece_out = lax.dynamic_update_slice_in_dim(piece_out, x_new, item_now * then, axis=0)
+        prior = arr_now
+        c += 1
+    return piece_out
 
 
 def from_behind(value, axis, steps):
@@ -115,10 +138,15 @@
     passed, finished = lax.fori_loop(0, blocks + sections - 1, advance, start)
     resident_embeddings = key_head(finished.reshape(group_images, width), final_norm_gain, w_head)
     momentum_embeddings = broadcast(resident_embeddings, "section", sections - 1)
-    query_rows_full = lax.all_gather(online_embeddings, "dp", axis=0, tiled=True)
     share = queue.shape[0]
     similarity_matrix = (
-        jnp.einsum("tw,fw->tf", query_rows_full, queue, preferred_element_type=jnp.float32)
+        lay_group_by_axis(
+            online_embeddings,
+            "dp",
+            lambda own_block, offset: jnp.einsum(
+                "tw,fw->tf", own_block, queue, preferred_element_type=jnp.float32
+            ),
+        )
         / contrastive_sharpness
     )
     local_peak = jnp.max(similarity_matrix, axis=1)

time: 524 us -> 531 us (1.013)
  waiting for transfers between devices: 14.3 us -> 50.6 us
  blocking collectives: 190 us -> 155 us
    ppermute x0 -> x7, waiting for transfers between devices: none -> 36.3 us  [lay_group_by_axis(): ppermute(prior, named_axis, row_list)]
    all_gather x1 -> x0, blocking collectives: 30.6 us -> none  [on_device(): lax.all_gather(online_embeddings, 'dp', axis=0, tiled=True)]
  transfers between devices with their start and end apart: 11 -> 18, of which waited for: 11 -> 17; matrix products, arithmetic and copies ran while one was open for 0% -> 36% of each run, Pallas kernels for 0% -> 0%
where the time goes in v1:
time: 531 us; the launch traced here: 529 us
  blocking collectives  155 us (29%)
  matrix products  131 us (25%)
  starting transfers between devices  120 us (23%)
  waiting for transfers between devices  50.6 us (10%)
  other arithmetic  40.7 us (8%)
  local copies, waits for them, and re-layouts  27.6 us (5%)
    ppermute x11, starting transfers between devices, from_behind(): lax.ppermute(value, axis, [(source, source + steps) for source in range(i...  117 us
    dot_general x8, matrix products, encoder_block(): jnp.dot(inner, second_weight, preferred_element_type=jnp.float32)  70 us
    dot_general x8, matrix products, encoder_block(): jnp.dot(normed, qkv_weight, preferred_element_type=jnp.float32)  43.2 us
    psum x1, blocking collectives, on_device(): lax.psum(jnp.sum(jnp.exp(similarity_matrix - top[:, None]), axis=1), ('dp...  41.2 us
    pmax x1, blocking collectives, on_device(): top = lax.pmax(local_peak, ('dp', 'section'))  36.9 us
    ppermute x7, waiting for transfers between devices, lay_group_by_axis(): ppermute(prior, named_axis, row_list)  36.3 us
    all_gather x1, blocking collectives, on_device(): every_key = lax.all_gather(momentum_embeddings, 'dp', axis=0, tiled=True)  31.1 us
    psum x1, blocking collectives, broadcast(): return lax.psum(kept, axis)  24.5 us
  transfers between devices with their start and end apart: 18, of which 17 were waited for; matrix products, arithmetic and copies ran while one was open for 36% of the time, Pallas kernels for 0%

profile of v1, /device:TPU:0, one launch (start us, length us, event | category | flops | bytes accessed | tf_op | source)
XLA Modules:
  0.0 528.8 jit_solution(15056592170406225824)
XLA Ops:
  9.2 320.3 %while.17 = (s32[]{:T(128)}, bf16[1,197,1024]{2,1,0:T(8,128)(2,1)S(1)}, bf16[8,1,1024]{2,1,0:T(2,128)(2,1)S(1)}, s32[]{:T(128)}, pred[]{:T(512)}, /*index=5*/bf1...) while((s32[]{:T(128)}, ...), condition=%wide.region_9.10_spmd, body=%wide.region_0.9_spmd.sunk | while | flops 3499673600 | bytes 49231128 | solution.py:138
  10.4 22.1 %conditional.2 = (bf16[1,197,1024]{2,1,0:T(8,128)(2,1)S(1)}) conditional(s32[]{:T(128)} %convert_element_type.128, bf16[1,197,1024]{2,1,0:T(8,128)(2,1)S(1)} %bitcast_select_fusion.2, (bf16[1,197,1024]{2,1,0:T(8,128)(2,1)S(1)}, f32[1,1024]{1,0:T(1,128)S(1)}, bf16[1,1024,3072]{2,1,0:T(8,128)(2,1)}, bf16[1,1024,1024]{2,1,0:T(8,128)(2,1)}, ...), branch_computations={%region_1.1_spmd, %region_2.8_spmd} | conditional | flops 3499470848 | bytes 46394252 | solution.py:130
  23.7 8.7 %fusion.40 = bf16[1,197,1024]{2,1,0:T(8,128)(2,1)S(1)} fusion(f32[1,197,1024]{2,1,0:T(8,128)S(1)} %get-tuple-element.344, bf16[1,2048,1024]{2,1,0:T(8,128)(2,1)} %get-tuple-element.295, bf16[1,1024,2048]{2,1,0:T(8,128)(2,1)} %get-tuple-element.294, f32[1024]{0:T(1024)S(1)} %bitcast.107, f32[197]{0:T(256)S(1)} %add_rsqrt_fusion, ...), kind=kOutput, calls=%fused_computation.40 | convolution fusion | flops 1679990784 | bytes 9604648 | tf_op jit(solution)/shard_map/while/body/eval_jaxpr/cond/branch_1_fun/dot_general | solution.py:80
  36.2 22.1 %conditional.2 = (bf16[1,197,1024]{2,1,0:T(8,128)(2,1)S(1)}) conditional(s32[]{:T(128)} %convert_element_type.128, bf16[1,197,1024]{2,1,0:T(8,128)(2,1)S(1)} %bitcast_select_fusion.2, (bf16[1,197,1024]{2,1,0:T(8,128)(2,1)S(1)}, f32[1,1024]{1,0:T(1,128)S(1)}, bf16[1,1024,3072]{2,1,0:T(8,128)(2,1)}, bf16[1,1024,1024]{2,1,0:T(8,128)(2,1)}, ...), branch_computations={%region_1.1_spmd, %region_2.8_spmd} | conditional | flops 3499470848 | bytes 46394252 | solution.py:130
  49.6 8.7 %fusion.40 = bf16[1,197,1024]{2,1,0:T(8,128)(2,1)S(1)} fusion(f32[1,197,1024]{2,1,0:T(8,128)S(1)} %get-tuple-element.344, bf16[1,2048,1024]{2,1,0:T(8,128)(2,1)} %get-tuple-element.295, bf16[1,1024,2048]{2,1,0:T(8,128)(2,1)} %get-tuple-element.294, f32[1024]{0:T(1024)S(1)} %bitcast.107, f32[197]{0:T(256)S(1)} %add_rsqrt_fusion, ...), kind=kOutput, calls=%fused_computation.40 | convolution fusion | flops 1679990784 | bytes 9604648 | tf_op jit(solution)/shard_map/while/body/eval_jaxpr/cond/branch_1_fun/dot_general | solution.py:80
  63.0 22.1 %conditional.2 = (bf16[1,197,1024]{2,1,0:T(8,128)(2,1)S(1)}) conditional(s32[]{:T(128)} %convert_element_type.128, bf16[1,197,1024]{2,1,0:T(8,128)(2,1)S(1)} %bitcast_select_fusion.2, (bf16[1,197,1024]{2,1,0:T(8,128)(2,1)S(1)}, f32[1,1024]{1,0:T(1,128)S(1)}, bf16[1,1024,3072]{2,1,0:T(8,128)(2,1)}, bf16[1,1024,1024]{2,1,0:T(8,128)(2,1)}, ...), branch_computations={%region_1.1_spmd, %region_2.8_spmd} | conditional | flops 3499470848 | bytes 46394252 | solution.py:130
  76.4 8.7 %fusion.40 = bf16[1,197,1024]{2,1,0:T(8,128)(2,1)S(1)} fusion(f32[1,197,1024]{2,1,0:T(8,128)S(1)} %get-tuple-element.344, bf16[1,2048,1024]{2,1,0:T(8,128)(2,1)} %get-tuple-element.295, bf16[1,1024,2048]{2,1,0:T(8,128)(2,1)} %get-tuple-element.294, f32[1024]{0:T(1024)S(1)} %bitcast.107, f32[197]{0:T(256)S(1)} %add_rsqrt_fusion, ...), kind=kOutput, calls=%fused_computation.40 | convolution fusion | flops 1679990784 | bytes 9604648 | tf_op jit(solution)/shard_map/while/body/eval_jaxpr/cond/branch_1_fun/dot_general | solution.py:80
  93.0 22.1 %conditional.2 = (bf16[1,197,1024]{2,1,0:T(8,128)(2,1)S(1)}) conditional(s32[]{:T(128)} %convert_element_type.128, bf16[1,197,1024]{2,1,0:T(8,128)(2,1)S(1)} %bitcast_select_fusion.2, (bf16[1,197,1024]{2,1,0:T(8,128)(2,1)S(1)}, f32[1,1024]{1,0:T(1,128)S(1)}, bf16[1,1024,3072]{2,1,0:T(8,128)(2,1)}, bf16[1,1024,1024]{2,1,0:T(8,128)(2,1)}, ...), branch_computations={%region_1.1_spmd, %region_2.8_spmd} | conditional | flops 3499470848 | bytes 46394252 | solution.py:130
  106.4 8.7 %fusion.40 = bf16[1,197,1024]{2,1,0:T(8,128)(2,1)S(1)} fusion(f32[1,197,1024]{2,1,0:T(8,128)S(1)} %get-tuple-element.344, bf16[1,2048,1024]{2,1,0:T(8,128)(2,1)} %get-tuple-element.295, bf16[1,1024,2048]{2,1,0:T(8,128)(2,1)} %get-tuple-element.294, f32[1024]{0:T(1024)S(1)} %bitcast.107, f32[197]{0:T(256)S(1)} %add_rsqrt_fusion, ...), kind=kOutput, calls=%fused_computation.40 | convolution fusion | flops 1679990784 | bytes 9604648 | tf_op jit(solution)/shard_map/while/body/eval_jaxpr/cond/branch_1_fun/dot_general | solution.py:80
  115.2 7.9 %collective-permute-start = (bf16[1,197,1024]{2,1,0:T(8,128)(2,1)S(1)}, bf16[1,197,1024]{2,1,0:T(8,128)(2,1)S(1)}, u32[]{:S(2)}, u32[]{:S(2)}) collective-permute-start(bf16[1,197,1024]{2,1,0:T(8,128)(2,1)S(1)} %get-tuple-element.474), channel_id=1, source_target_pairs={{0,1},{1,2},{2,3},{4,5},{5,6},{6,7},{8,9},{9,10},{10,11},{12,13},{... | collective-permute-start | bytes 1210376 | tf_op jit(solution)/shard_map/while/body/eval_jaxpr/ppermute | solution.py:40
  125.5 22.1 %conditional.2 = (bf16[1,197,1024]{2,1,0:T(8,128)(2,1)S(1)}) conditional(s32[]{:T(128)} %convert_element_type.128, bf16[1,197,1024]{2,1,0:T(8,128)(2,1)S(1)} %bitcast_select_fusion.2, (bf16[1,197,1024]{2,1,0:T(8,128)(2,1)S(1)}, f32[1,1024]{1,0:T(1,128)S(1)}, bf16[1,1024,3072]{2,1,0:T(8,128)(2,1)}, bf16[1,1024,1024]{2,1,0:T(8,128)(2,1)}, ...), branch_computations={%region_1.1_spmd, %region_2.8_spmd} | conditional | flops 3499470848 | bytes 46394252 | solution.py:130
  138.9 8.7 %fusion.40 = bf16[1,197,1024]{2,1,0:T(8,128)(2,1)S(1)} fusion(f32[1,197,1024]{2,1,0:T(8,128)S(1)} %get-tuple-element.344, bf16[1,2048,1024]{2,1,0:T(8,128)(2,1)} %get-tuple-element.295, bf16[1,1024,2048]{2,1,0:T(8,128)(2,1)} %get-tuple-element.294, f32[1024]{0:T(1024)S(1)} %bitcast.107, f32[197]{0:T(256)S(1)} %add_rsqrt_fusion, ...), kind=kOutput, calls=%fused_computation.40 | convolution fusion | flops 1679990784 | bytes 9604648 | tf_op jit(solution)/shard_map/while/body/eval_jaxpr/cond/branch_1_fun/dot_general | solution.py:80
  147.6 7.9 %collective-permute-start = (bf16[1,197,1024]{2,1,0:T(8,128)(2,1)S(1)}, bf16[1,197,1024]{2,1,0:T(8,128)(2,1)S(1)}, u32[]{:S(2)}, u32[]{:S(2)}) collective-permute-start(bf16[1,197,1024]{2,1,0:T(8,128)(2,1)S(1)} %get-tuple-element.474), channel_id=1, source_target_pairs={{0,1},{1,2},{2,3},{4,5},{5,6},{6,7},{8,9},{9,10},{10,11},{12,13},{... | collective-permute-start | bytes 1210376 | tf_op jit(solution)/shard_map/while/body/eval_jaxpr/ppermute | solution.py:40
  157.9 22.1 %conditional.2 = (bf16[1,197,1024]{2,1,0:T(8,128)(2,1)S(1)}) conditional(s32[]{:T(128)} %convert_element_type.128, bf16[1,197,1024]{2,1,0:T(8,128)(2,1)S(1)} %bitcast_select_fusion.2, (bf16[1,197,1024]{2,1,0:T(8,128)(2,1)S(1)}, f32[1,1024]{1,0:T(1,128)S(1)}, bf16[1,1024,3072]{2,1,0:T(8,128)(2,1)}, bf16[1,1024,1024]{2,1,0:T(8,128)(2,1)}, ...), branch_computations={%region_1.1_spmd, %region_2.8_spmd} | conditional | flops 3499470848 | bytes 46394252 | solution.py:130
  171.3 8.7 %fusion.40 = bf16[1,197,1024]{2,1,0:T(8,128)(2,1)S(1)} fusion(f32[1,197,1024]{2,1,0:T(8,128)S(1)} %get-tuple-element.344, bf16[1,2048,1024]{2,1,0:T(8,128)(2,1)} %get-tuple-element.295, bf16[1,1024,2048]{2,1,0:T(8,128)(2,1)} %get-tuple-element.294, f32[1024]{0:T(1024)S(1)} %bitcast.107, f32[197]{0:T(256)S(1)} %add_rsqrt_fusion, ...), kind=kOutput, calls=%fused_computation.40 | convolution fusion | flops 1679990784 | bytes 9604648 | tf_op jit(solution)/shard_map/while/body/eval_jaxpr/cond/branch_1_fun/dot_general | solution.py:80
  180.1 7.9 %collective-permute-start = (bf16[1,197,1024]{2,1,0:T(8,128)(2,1)S(1)}, bf16[1,197,1024]{2,1,0:T(8,128)(2,1)S(1)}, u32[]{:S(2)}, u32[]{:S(2)}) collective-permute-start(bf16[1,197,1024]{2,1,0:T(8,128)(2,1)S(1)} %get-tuple-element.474), channel_id=1, source_target_pairs={{0,1},{1,2},{2,3},{4,5},{5,6},{6,7},{8,9},{9,10},{10,11},{12,13},{... | collective-permute-start | bytes 1210376 | tf_op jit(solution)/shard_map/while/body/eval_jaxpr/ppermute | solution.py:40
  190.4 22.1 %conditional.2 = (bf16[1,197,1024]{2,1,0:T(8,128)(2,1)S(1)}) conditional(s32[]{:T(128)} %convert_element_type.128, bf16[1,197,1024]{2,1,0:T(8,128)(2,1)S(1)} %bitcast_select_fusion.2, (bf16[1,197,1024]{2,1,0:T(8,128)(2,1)S(1)}, f32[1,1024]{1,0:T(1,128)S(1)}, bf16[1,1024,3072]{2,1,0:T(8,128)(2,1)}, bf16[1,1024,1024]{2,1,0:T(8,128)(2,1)}, ...), branch_computations={%region_1.1_spmd, %region_2.8_spmd} | conditional | flops 3499470848 | bytes 46394252 | solution.py:130
  203.8 8.7 %fusion.40 = bf16[1,197,1024]{2,1,0:T(8,128)(2,1)S(1)} fusion(f32[1,197,1024]{2,1,0:T(8,128)S(1)} %get-tuple-element.344, bf16[1,2048,1024]{2,1,0:T(8,128)(2,1)} %get-tuple-element.295, bf16[1,1024,2048]{2,1,0:T(8,128)(2,1)} %get-tuple-element.294, f32[1024]{0:T(1024)S(1)} %bitcast.107, f32[197]{0:T(256)S(1)} %add_rsqrt_fusion, ...), kind=kOutput, calls=%fused_computation.40 | convolution fusion | flops 1679990784 | bytes 9604648 | tf_op jit(solution)/shard_map/while/body/eval_jaxpr/cond/branch_1_fun/dot_general | solution.py:80
  212.5 7.9 %collective-permute-start = (bf16[1,197,1024]{2,1,0:T(8,128)(2,1)S(1)}, bf16[1,197,1024]{2,1,0:T(8,128)(2,1)S(1)}, u32[]{:S(2)}, u32[]{:S(2)}) collective-permute-start(bf16[1,197,1024]{2,1,0:T(8,128)(2,1)S(1)} %get-tuple-element.474), channel_id=1, source_target_pairs={{0,1},{1,2},{2,3},{4,5},{5,6},{6,7},{8,9},{9,10},{10,11},{12,13},{... | collective-permute-start | bytes 1210376 | tf_op jit(solution)/shard_map/while/body/eval_jaxpr/ppermute | solution.py:40
  222.8 22.1 %conditional.2 = (bf16[1,197,1024]{2,1,0:T(8,128)(2,1)S(1)}) conditional(s32[]{:T(128)} %convert_element_type.128, bf16[1,197,1024]{2,1,0:T(8,128)(2,1)S(1)} %bitcast_select_fusion.2, (bf16[1,197,1024]{2,1,0:T(8,128)(2,1)S(1)}, f32[1,1024]{1,0:T(1,128)S(1)}, bf16[1,1024,3072]{2,1,0:T(8,128)(2,1)}, bf16[1,1024,1024]{2,1,0:T(8,128)(2,1)}, ...), branch_computations={%region_1.1_spmd, %region_2.8_spmd} | conditional | flops 3499470848 | bytes 46394252 | solution.py:130
  236.2 8.7 %fusion.40 = bf16[1,197,1024]{2,1,0:T(8,128)(2,1)S(1)} fusion(f32[1,197,1024]{2,1,0:T(8,128)S(1)} %get-tuple-element.344, bf16[1,2048,1024]{2,1,0:T(8,128)(2,1)} %get-tuple-element.295, bf16[1,1024,2048]{2,1,0:T(8,128)(2,1)} %get-tuple-element.294, f32[1024]{0:T(1024)S(1)} %bitcast.107, f32[197]{0:T(256)S(1)} %add_rsqrt_fusion, ...), kind=kOutput, calls=%fused_computation.40 | convolution fusion | flops 1679990784 | bytes 9604648 | tf_op jit(solution)/shard_map/while/body/eval_jaxpr/cond/branch_1_fun/dot_general | solution.py:80
  245.0 7.9 %collective-permute-start = (bf16[1,197,1024]{2,1,0:T(8,128)(2,1)S(1)}, bf16[1,197,1024]{2,1,0:T(8,128)(2,1)S(1)}, u32[]{:S(2)}, u32[]{:S(2)}) collective-permute-start(bf16[1,197,1024]{2,1,0:T(8,128)(2,1)S(1)} %get-tuple-element.474), channel_id=1, source_target_pairs={{0,1},{1,2},{2,3},{4,5},{5,6},{6,7},{8,9},{9,10},{10,11},{12,13},{... | collective-permute-start | bytes 1210376 | tf_op jit(solution)/shard_map/while/body/eval_jaxpr/ppermute | solution.py:40
  255.3 30.1 %collective-permute-start = (bf16[1,197,1024]{2,1,0:T(8,128)(2,1)S(1)}, bf16[1,197,1024]{2,1,0:T(8,128)(2,1)S(1)}, u32[]{:S(2)}, u32[]{:S(2)}) collective-permute-start(bf16[1,197,1024]{2,1,0:T(8,128)(2,1)S(1)} %get-tuple-element.474), channel_id=1, source_target_pairs={{0,1},{1,2},{2,3},{4,5},{5,6},{6,7},{8,9},{9,10},{10,11},{12,13},{... | collective-permute-start | bytes 1210376 | tf_op jit(solution)/shard_map/while/body/eval_jaxpr/ppermute | solution.py:40
  287.8 7.9 %collective-permute-start = (bf16[1,197,1024]{2,1,0:T(8,128)(2,1)S(1)}, bf16[1,197,1024]{2,1,0:T(8,128)(2,1)S(1)}, u32[]{:S(2)}, u32[]{:S(2)}) collective-permute-start(bf16[1,197,1024]{2,1,0:T(8,128)(2,1)S(1)} %get-tuple-element.474), channel_id=1, source_target_pairs={{0,1},{1,2},{2,3},{4,5},{5,6},{6,7},{8,9},{9,10},{10,11},{12,13},{... | collective-permute-start | bytes 1210376 | tf_op jit(solution)/shard_map/while/body/eval_jaxpr/ppermute | solution.py:40
  298.1 30.1 %collective-permute-start = (bf16[1,197,1024]{2,1,0:T(8,128)(2,1)S(1)}, bf16[1,197,1024]{2,1,0:T(8,128)(2,1)S(1)}, u32[]{:S(2)}, u32[]{:S(2)}) collective-permute-start(bf16[1,197,1024]{2,1,0:T(8,128)(2,1)S(1)} %get-tuple-element.474), channel_id=1, source_target_pairs={{0,1},{1,2},{2,3},{4,5},{5,6},{6,7},{8,9},{9,10},{10,11},{12,13},{... | collective-permute-start | bytes 1210376 | tf_op jit(solution)/shard_map/while/body/eval_jaxpr/ppermute | solution.py:40
  330.3 24.5 %psum.21 = bf16[8,256]{1,0:T(8,128)(2,1)S(1)} all-reduce(bf16[8,256]{1,0:T(8,128)(2,1)S(1)} %fusion.136), channel_id=1, replica_groups=mesh['dp'=8,'section'=4] {'section'}, use_global_device_ids=true, to_apply=%region_13.14 | all-reduce | flops 2048 | bytes 8192 | tf_op jit(solution)/shard_map/psum | solution.py:45
  355.0 31.1 %all_gather.3 = bf16[64,256]{1,0:T(8,128)(2,1)S(1)} all-gather(bf16[8,256]{1,0:T(8,128)(2,1)S(1)} %psum.21), channel_id=1, replica_groups=mesh['dp'=8,'section'=4] {'dp'}, dimensions={0}, use_global_device_ids=true | all-gather | bytes 36864 | tf_op jit(solution)/shard_map/all_gather | solution.py:171
  407.5 6.1 %collective-permute-done.5 = bf16[8,256]{1,0:T(8,128)(2,1)S(1)} collective-permute-done((bf16[8,256]{1,0:T(8,128)(2,1)S(1)}, bf16[8,256]{1,0:T(8,128)(2,1)S(1)}, u32[]{:S(2)}, u32[]{:S(2)}) %collective-permute-start.5) | collective-permute-done | bytes 4128 | tf_op jit(solution)/shard_map/ppermute | solution.py:24
  413.8 6.1 %collective-permute-done.6 = bf16[8,256]{1,0:T(8,128)(2,1)S(1)} collective-permute-done((bf16[8,256]{1,0:T(8,128)(2,1)S(1)}, bf16[8,256]{1,0:T(8,128)(2,1)S(1)}, u32[]{:S(2)}, u32[]{:S(2)}) %collective-permute-start.6) | collective-permute-done | bytes 4128 | tf_op jit(solution)/shard_map/ppermute | solution.py:24
  426.5 36.9 %pmax.7 = f32[64]{0:T(128)S(1)} all-reduce(f32[64]{0:T(128)S(1)} %multiply_reduce_fusion.2), channel_id=1, replica_groups=mesh['dp'=8,'section'=4] {'dp','section'}, use_global_device_ids=true, to_apply=%region_15.16 | all-reduce | flops 64 | bytes 512 | tf_op jit(solution)/shard_map/pmax | solution.py:153
  463.6 41.2 %psum.22 = f32[64]{0:T(128)S(1)} all-reduce(f32[64]{0:T(128)S(1)} %exponential_reduce_fusion), channel_id=1, replica_groups=mesh['dp'=8,'section'=4] {'dp','section'}, use_global_device_ids=true, to_apply=%region_17.18 | all-reduce | flops 64 | bytes 512 | tf_op jit(solution)/shard_map/psum | solution.py:154
  506.0 21.0 %psum.23 = f32[]{:T(128)} all-reduce(f32[]{:T(128)} %get-tuple-element.339), channel_id=1, replica_groups=mesh['dp'=8,'section'=4] {'dp'}, use_global_device_ids=true, to_apply=%region_20.21 | all-reduce | flops 1 | bytes 8 | tf_op jit(solution)/shard_map/psum | solution.py:169
  (216 shorter events, 180.3 us)
Async XLA Ops:
  0.6 329.3 %copy-start = (bf16[1024,256]{1,0:T(8,128)(2,1)S(1)}, bf16[1024,256]{1,0:T(8,128)(2,1)}, u32[]{:S(2)}) copy-start(bf16[1024,256]{1,0:T(8,128)(2,1)} %param.25) | copy-start | bytes 1572868
  0.6 387.7 %collective-permute-start.1 = (bf16[8,256]{1,0:T(8,128)(2,1)}, bf16[8,256]{1,0:T(8,128)(2,1)S(1)}, u32[]{:S(2)}, u32[]{:S(2)}) collective-permute-start(bf16[8,256]{1,0:T(8,128)(2,1)} %param.26), channel_id=1, source_target_pairs={{0,4},{4,8},{8,12},{12,16},{16,20},{20,24},{24,28},{28,0},{1,5},{5... | collective-permute-start | bytes 12296 | tf_op jit(solution)/shard_map/ppermute | solution.py:24
  3.7 5.5 %copy-start.6 = (f32[1,1024]{1,0:T(1,128)S(1)}, f32[1,1024]{1,0:T(1,128)}, u32[]{:S(2)}) copy-start(f32[1,1024]{1,0:T(1,128)} %param.18) | copy-start | bytes 12292
  3.7 5.5 %copy-start.7 = (f32[1,1024]{1,0:T(1,128)S(1)}, f32[1,1024]{1,0:T(1,128)}, u32[]{:S(2)}) copy-start(f32[1,1024]{1,0:T(1,128)} %param.21) | copy-start | bytes 12292
  9.2 320.7 %copy-start.8 = (f32[1024]{0:T(1024)S(1)}, f32[1024]{0:T(1024)}, u32[]{:S(2)}) copy-start(f32[1024]{0:T(1024)} %param.24) | copy-start | bytes 12292
  9.2 345.6 %copy-start.4 = (bf16[8,256]{1,0:T(8,128)(2,1)S(1)}, bf16[8,256]{1,0:T(8,128)(2,1)}, u32[]{:S(2)}) copy-start(bf16[8,256]{1,0:T(8,128)(2,1)} %param.26) | copy-start | bytes 12292
  9.2 377.6 %copy-start.2 = (bf16[1024,256]{1,0:T(8,128)(2,1)S(1)}, bf16[1024,256]{1,0:T(8,128)(2,1)}, u32[]{:S(2)}) copy-start(bf16[1024,256]{1,0:T(8,128)(2,1)} %param.27) | copy-start | bytes 1572868
  21.2 1.6 copy-start.1
  32.5 2.7 collective-permute-start
  47.0 1.6 copy-start.1
  58.3 3.7 collective-permute-start
  73.9 1.6 copy-start.1
  85.2 6.8 %collective-permute-start = (bf16[1,197,1024]{2,1,0:T(8,128)(2,1)S(1)}, bf16[1,197,1024]{2,1,0:T(8,128)(2,1)S(1)}, u32[]{:S(2)}, u32[]{:S(2)}) collective-permute-start(bf16[1,197,1024]{2,1,0:T(8,128)(2,1)S(1)} %get-tuple-element.474), channel_id=1, source_target_pairs={{0,1},{1,2},{2,3},{4,5},{5,6},{6,7},{8,9},{9,10},{10,11},{12,13},{... | collective-permute-start | bytes 1210376 | tf_op jit(solution)/shard_map/while/body/eval_jaxpr/ppermute | solution.py:40
  115.2 9.3 %collective-permute-start = (bf16[1,197,1024]{2,1,0:T(8,128)(2,1)S(1)}, bf16[1,197,1024]{2,1,0:T(8,128)(2,1)S(1)}, u32[]{:S(2)}, u32[]{:S(2)}) collective-permute-start(bf16[1,197,1024]{2,1,0:T(8,128)(2,1)S(1)} %get-tuple-element.474), channel_id=1, source_target_pairs={{0,1},{1,2},{2,3},{4,5},{5,6},{6,7},{8,9},{9,10},{10,11},{12,13},{... | collective-permute-start | bytes 1210376 | tf_op jit(solution)/shard_map/while/body/eval_jaxpr/ppermute | solution.py:40
  136.3 1.6 copy-start.1
  147.6 9.3 %collective-permute-start = (bf16[1,197,1024]{2,1,0:T(8,128)(2,1)S(1)}, bf16[1,197,1024]{2,1,0:T(8,128)(2,1)S(1)}, u32[]{:S(2)}, u32[]{:S(2)}) collective-permute-start(bf16[1,197,1024]{2,1,0:T(8,128)(2,1)S(1)} %get-tuple-element.474), channel_id=1, source_target_pairs={{0,1},{1,2},{2,3},{4,5},{5,6},{6,7},{8,9},{9,10},{10,11},{12,13},{... | collective-permute-start | bytes 1210376 | tf_op jit(solution)/shard_map/while/body/eval_jaxpr/ppermute | solution.py:40
  168.8 1.6 copy-start.1
  180.1 9.3 %collective-permute-start = (bf16[1,197,1024]{2,1,0:T(8,128)(2,1)S(1)}, bf16[1,197,1024]{2,1,0:T(8,128)(2,1)S(1)}, u32[]{:S(2)}, u32[]{:S(2)}) collective-permute-start(bf16[1,197,1024]{2,1,0:T(8,128)(2,1)S(1)} %get-tuple-element.474), channel_id=1, source_target_pairs={{0,1},{1,2},{2,3},{4,5},{5,6},{6,7},{8,9},{9,10},{10,11},{12,13},{... | collective-permute-start | bytes 1210376 | tf_op jit(solution)/shard_map/while/body/eval_jaxpr/ppermute | solution.py:40
  201.2 1.6 copy-start.1
  212.5 9.3 %collective-permute-start = (bf16[1,197,1024]{2,1,0:T(8,128)(2,1)S(1)}, bf16[1,197,1024]{2,1,0:T(8,128)(2,1)S(1)}, u32[]{:S(2)}, u32[]{:S(2)}) collective-permute-start(bf16[1,197,1024]{2,1,0:T(8,128)(2,1)S(1)} %get-tuple-element.474), channel_id=1, source_target_pairs={{0,1},{1,2},{2,3},{4,5},{5,6},{6,7},{8,9},{9,10},{10,11},{12,13},{... | collective-permute-start | bytes 1210376 | tf_op jit(solution)/shard_map/while/body/eval_jaxpr/ppermute | solution.py:40
  245.0 9.3 %collective-permute-start = (bf16[1,197,1024]{2,1,0:T(8,128)(2,1)S(1)}, bf16[1,197,1024]{2,1,0:T(8,128)(2,1)S(1)}, u32[]{:S(2)}, u32[]{:S(2)}) collective-permute-start(bf16[1,197,1024]{2,1,0:T(8,128)(2,1)S(1)} %get-tuple-element.474), channel_id=1, source_target_pairs={{0,1},{1,2},{2,3},{4,5},{5,6},{6,7},{8,9},{9,10},{10,11},{12,13},{... | collective-permute-start | bytes 1210376 | tf_op jit(solution)/shard_map/while/body/eval_jaxpr/ppermute | solution.py:40
  255.3 31.4 %collective-permute-start = (bf16[1,197,1024]{2,1,0:T(8,128)(2,1)S(1)}, bf16[1,197,1024]{2,1,0:T(8,128)(2,1)S(1)}, u32[]{:S(2)}, u32[]{:S(2)}) collective-permute-start(bf16[1,197,1024]{2,1,0:T(8,128)(2,1)S(1)} %get-tuple-element.474), channel_id=1, source_target_pairs={{0,1},{1,2},{2,3},{4,5},{5,6},{6,7},{8,9},{9,10},{10,11},{12,13},{... | collective-permute-start | bytes 1210376 | tf_op jit(solution)/shard_map/while/body/eval_jaxpr/ppermute | solution.py:40
  287.8 9.3 %collective-permute-start = (bf16[1,197,1024]{2,1,0:T(8,128)(2,1)S(1)}, bf16[1,197,1024]{2,1,0:T(8,128)(2,1)S(1)}, u32[]{:S(2)}, u32[]{:S(2)}) collective-permute-start(bf16[1,197,1024]{2,1,0:T(8,128)(2,1)S(1)} %get-tuple-element.474), channel_id=1, source_target_pairs={{0,1},{1,2},{2,3},{4,5},{5,6},{6,7},{8,9},{9,10},{10,11},{12,13},{... | collective-permute-start | bytes 1210376 | tf_op jit(solution)/shard_map/while/body/eval_jaxpr/ppermute | solution.py:40
  298.1 31.4 %collective-permute-start = (bf16[1,197,1024]{2,1,0:T(8,128)(2,1)S(1)}, bf16[1,197,1024]{2,1,0:T(8,128)(2,1)S(1)}, u32[]{:S(2)}, u32[]{:S(2)}) collective-permute-start(bf16[1,197,1024]{2,1,0:T(8,128)(2,1)S(1)} %get-tuple-element.474), channel_id=1, source_target_pairs={{0,1},{1,2},{2,3},{4,5},{5,6},{6,7},{8,9},{9,10},{10,11},{12,13},{... | collective-permute-start | bytes 1210376 | tf_op jit(solution)/shard_map/while/body/eval_jaxpr/ppermute | solution.py:40
  329.5 57.5 %copy-start.5 = (s32[64]{0:T(128)S(1)}, s32[64]{0:T(128)}, u32[]{:S(2)}) copy-start(s32[64]{0:T(128)} %param.28) | copy-start | bytes 772
  354.8 46.4 %copy-start.3 = (bf16[8,256]{1,0:T(8,128)(2,1)}, bf16[8,256]{1,0:T(8,128)(2,1)S(1)}, u32[]{:S(2)}) copy-start(bf16[8,256]{1,0:T(8,128)(2,1)S(1)} %psum.21) | copy-start | bytes 12292
  388.3 6.3 %collective-permute-start.2 = (bf16[8,256]{1,0:T(8,128)(2,1)S(1)}, bf16[8,256]{1,0:T(8,128)(2,1)S(1)}, u32[]{:S(2)}, u32[]{:S(2)}) collective-permute-start(bf16[8,256]{1,0:T(8,128)(2,1)S(1)} %collective-permute-done.1), channel_id=1, source_target_pairs={{0,4},{4,8},{8,12},{12,16},{16,20},{20,24},{24,28},{28,0},{1,5},{5... | collective-permute-start | bytes 12296 | tf_op jit(solution)/shard_map/ppermute | solution.py:24
  394.6 6.3 %collective-permute-start.3 = (bf16[8,256]{1,0:T(8,128)(2,1)S(1)}, bf16[8,256]{1,0:T(8,128)(2,1)S(1)}, u32[]{:S(2)}, u32[]{:S(2)}) collective-permute-start(bf16[8,256]{1,0:T(8,128)(2,1)S(1)} %collective-permute-done.2), channel_id=1, source_target_pairs={{0,4},{4,8},{8,12},{12,16},{16,20},{20,24},{24,28},{28,0},{1,5},{5... | collective-permute-start | bytes 12296 | tf_op jit(solution)/shard_map/ppermute | solution.py:24
  400.9 6.3 %collective-permute-start.4 = (bf16[8,256]{1,0:T(8,128)(2,1)S(1)}, bf16[8,256]{1,0:T(8,128)(2,1)S(1)}, u32[]{:S(2)}, u32[]{:S(2)}) collective-permute-start(bf16[8,256]{1,0:T(8,128)(2,1)S(1)} %collective-permute-done.3), channel_id=1, source_target_pairs={{0,4},{4,8},{8,12},{12,16},{16,20},{20,24},{24,28},{28,0},{1,5},{5... | collective-permute-start | bytes 12296 | tf_op jit(solution)/shard_map/ppermute | solution.py:24
  407.3 6.3 %collective-permute-start.5 = (bf16[8,256]{1,0:T(8,128)(2,1)S(1)}, bf16[8,256]{1,0:T(8,128)(2,1)S(1)}, u32[]{:S(2)}, u32[]{:S(2)}) collective-permute-start(bf16[8,256]{1,0:T(8,128)(2,1)S(1)} %collective-permute-done.4), channel_id=1, source_target_pairs={{0,4},{4,8},{8,12},{12,16},{16,20},{20,24},{24,28},{28,0},{1,5},{5... | collective-permute-start | bytes 12296 | tf_op jit(solution)/shard_map/ppermute | solution.py:24
  413.6 6.3 %collective-permute-start.6 = (bf16[8,256]{1,0:T(8,128)(2,1)S(1)}, bf16[8,256]{1,0:T(8,128)(2,1)S(1)}, u32[]{:S(2)}, u32[]{:S(2)}) collective-permute-start(bf16[8,256]{1,0:T(8,128)(2,1)S(1)} %collective-permute-done.5), channel_id=1, source_target_pairs={{0,4},{4,8},{8,12},{12,16},{16,20},{20,24},{24,28},{28,0},{1,5},{5... | collective-permute-start | bytes 12296 | tf_op jit(solution)/shard_map/ppermute | solution.py:24
  419.9 6.3 %collective-permute-start.7 = (bf16[8,256]{1,0:T(8,128)(2,1)S(1)}, bf16[8,256]{1,0:T(8,128)(2,1)S(1)}, u32[]{:S(2)}, u32[]{:S(2)}) collective-permute-start(bf16[8,256]{1,0:T(8,128)(2,1)S(1)} %collective-permute-done.6), channel_id=1, source_target_pairs={{0,4},{4,8},{8,12},{12,16},{16,20},{20,24},{24,28},{28,0},{1,5},{5... | collective-permute-start | bytes 12296 | tf_op jit(solution)/shard_map/ppermute | solution.py:24
  (2 other events, 3.2 us)
